TPU v7x, 32 devices: a whole 2x2x4 slice. The times are simulated.
32 devices in a mesh: row: 4 (over y, x), col: 8 (over z, core).
Axes of the slice: x: 2, y: 2, z: 4, core: 2. Of those that a mesh axis runs over, the one named last changes fastest.
Arguments:
- layer_input: bfloat16 [8192, 2048], P(('row', 'col')), may hold values from -6 to 6
- out_grad: bfloat16 [8192, 2048], P(('row', 'col')), may hold values from -6 to 6
- kv_grad: bfloat16 [8192, 256], P(('row', 'col')), may hold values from -6 to 6
- lengths: int32 [4, 4], P('row'), may hold values from 1 to 1024, 2048 in all within a row
- token_deal: int32 [4, 2048], P('row'), may hold values from 0 to 2047, each once within a row
- attn_gain: float32 [2048], P('row'), may hold values from 0.25 to 1.75
- query_weight: float32 [2048, 2048], P('row', 'col'), may hold values from -0.125 to 0.125
- key_weight: float32 [2048, 128], P('row'), may hold values from -0.125 to 0.125
- value_weight: float32 [2048, 128], P('row'), may hold values from -0.125 to 0.125
- out_weight: float32 [2048, 2048], P('col', 'row'), may hold values from -1 to 1
- mlp_gain: float32 [2048], P('row'), may hold values from 0.25 to 1.75
- gate_weight: float32 [2048, 5632], P('row', 'col'), may hold values from -0.125 to 0.125
- up_weight: float32 [2048, 5632], P('row', 'col'), may hold values from -0.125 to 0.125
- down_weight: float32 [5632, 2048], P('col', 'row'), may hold values from -0.3125 to 0.3125
Outputs:
- layer_output: bfloat16 [8192, 2048], P(('row', 'col'))
- input_grad: float32 [8192, 2048], P(('row', 'col'))
- shared_kv: bfloat16 [8192, 256], P(('row', 'col'))
- attn_gain_grad: float32 [2048], P('row')
- query_weight_grad: float32 [2048, 2048], P('row', 'col')
- key_weight_grad: float32 [2048, 128], P('row')
- value_weight_grad: float32 [2048, 128], P('row')
- out_weight_grad: float32 [2048, 2048], P('col', 'row')
- mlp_gain_grad: float32 [2048], P('row')
- gate_weight_grad: float32 [2048, 5632], P('row', 'col')
- up_weight_grad: float32 [2048, 5632], P('row', 'col')
- down_weight_grad: float32 [5632, 2048], P('col', 'row')
Inputs may be any that keep to these rules, and one draw needn't show every extreme that they name: Each row holds 4 lengths that sum to 2048; the longest of each row is exactly 1024. `token_deal`: each row is a permutation of 0 to 2047.
All inputs are finite; a program needn't handle non-finite values.
Results may differ from a plain program's by a relative error of at most 0.017.
The roundings to bfloat16 on the way count: a program that leaves them out, or rounds other values in their place, can miss the bound.
Values may be sent and summed in bfloat16 or wider, within the bound.
No kernel may reach another device: no remote copies, remote signals or barrier semaphores. Data moves between devices by JAX's collectives and lax.ppermute only.
A program may use at most 320 MiB of HBM per device.

v0:
```python
import jax
import jax.numpy as jnp
from jax import lax
from jax.sharding import PartitionSpec as P

norm_eps = 1e-05
rope_base = 10000.0
masked_score = -1e30


def rotate_pairs(values, positions, direction):
    half_dim = values.shape[-1] // 2
    frequency = rope_base ** (-jnp.arange(half_dim, dtype=jnp.float32) / half_dim)
    angles = positions.astype(jnp.float32)[:, None, None] * frequency
    cosine = jnp.cos(angles)
    sine_part = jnp.sin(angles) * direction
    first_half = values[..., :half_dim]
    second = values[..., half_dim:]
    return jnp.concatenate(
        [first_half * cosine - second * sine_part, second * cosine + first_half * sine_part],
        axis=-1,
    )


def norm_parts(values, gain):
    factor = lax.rsqrt(jnp.mean(values * values, axis=-1, keepdims=True) + norm_eps)
    return (factor, values * factor * gain)


def norm_backward(values, factor, gain, grad_rows):
    weighted = grad_rows * gain
    inner_mean = jnp.mean(weighted * values, axis=-1, keepdims=True)
    input_part = factor * weighted - values * factor * factor * factor * inner_mean
    gain_part = jnp.sum(grad_rows * values * factor, axis=0)
    return (input_part, gain_part)


def sequence_info(seq_lengths, group_rows):
    positions = jnp.arange(group_rows, dtype=jnp.int32)
    seq_ends = jnp.cumsum(seq_lengths)
    seq_ids = jnp.sum((positions[:, None] >= seq_ends[None, :]).astype(jnp.int32), axis=1)
    starts = jnp.sum(
        jnp.where(seq_ends[None, :] <= positions[:, None], seq_lengths[None, :], 0), axis=1
    )
    return (positions, seq_ids, positions - starts)


def block_scores(query_block, key_rows, seq_ids, first_row, block_rows, score_scale):
    key_index = jnp.arange(key_rows.shape[0], dtype=jnp.int32)
    row_index = first_row + jnp.arange(block_rows, dtype=jnp.int32)
    row_seq = lax.dynamic_slice_in_dim(seq_ids, first_row, block_rows, 0)
    scores = (
        jnp.einsum("qhd,kd->hqk", query_block, key_rows, preferred_element_type=jnp.float32)
        * score_scale
    )
    allowed = (row_seq[:, None] == seq_ids[None, :]) & (key_index[None, :] <= row_index[:, None])
    return jnp.where(allowed[None], scores, masked_score)


def attend_forward(queries, key_rows, value_rows, seq_ids):
    group_rows, head_count, head_dim = queries.shape
    block_rows = min(512, group_rows)
    score_scale = float(head_dim) ** (-0.5)
    count_blocks = group_rows // block_rows
    query_blocks = queries.reshape(count_blocks, block_rows, head_count, head_dim)
    first_rows = jnp.arange(count_blocks, dtype=jnp.int32) * block_rows

    def one_block(pieces):
        query_block, first_row = pieces
        scores = block_scores(query_block, key_rows, seq_ids, first_row, block_rows, score_scale)
        highest = jnp.max(scores, axis=-1, keepdims=True)
        exponent = jnp.exp(scores - highest)
        row_total = jnp.sum(exponent, axis=-1, keepdims=True)
        prob_low = (exponent / row_total).astype(jnp.bfloat16)
        mixed_rows = jnp.einsum(
            "hqk,kd->qhd", prob_low, value_rows, preferred_element_type=jnp.float32
        )
        return (mixed_rows.astype(jnp.bfloat16), (highest + jnp.log(row_total))[..., 0])

    mixed_rows, log_norm = lax.map(one_block, (query_blocks, first_rows))
    return (mixed_rows.reshape(group_rows, head_count, head_dim), log_norm)


def attend_backward(queries, key_rows, value_rows, seq_ids, mixed_grad, log_norm):
    group_rows, head_count, head_dim = queries.shape
    block_rows = min(512, group_rows)
    score_scale = float(head_dim) ** (-0.5)
    count_blocks = group_rows // block_rows
    query_blocks = queries.reshape(count_blocks, block_rows, head_count, head_dim)
    grad_blocks = mixed_grad.reshape(count_blocks, block_rows, head_count, head_dim)
    first_rows = jnp.arange(count_blocks, dtype=jnp.int32) * block_rows

    def one_block(carry, pieces):
        key_grad, value_grad = carry
        query_block, grad_block, norm_block, first_row = pieces
        scores = block_scores(query_block, key_rows, seq_ids, first_row, block_rows, score_scale)
        softmax_rows = jnp.exp(scores - norm_block[..., None])
        prob_low = softmax_rows.astype(jnp.bfloat16)
        prob_grad = jnp.einsum(
            "qhd,kd->hqk", grad_block, value_rows, preferred_element_type=jnp.float32
        )
        row_dot = jnp.sum(softmax_rows * prob_grad, axis=-1, keepdims=True)
        score_grad = (softmax_rows * (prob_grad - row_dot)).astype(jnp.bfloat16)
        query_grad = (
            jnp.einsum("hqk,kd->qhd", score_grad, key_rows, preferred_element_type=jnp.float32)
            * score_scale
        )
        key_grad = (
            key_grad
            + jnp.einsum("hqk,qhd->kd", score_grad, query_block, preferred_element_type=jnp.float32)
            * score_scale
        )
        value_grad = value_grad + jnp.einsum(
            "hqk,qhd->kd", prob_low, grad_block, preferred_element_type=jnp.float32
        )
        return ((key_grad, value_grad), query_grad)

    zero_rows = jnp.zeros((group_rows, head_dim), jnp.float32)
    (key_grad, value_grad), query_grad = lax.scan(
        one_block, (zero_rows, zero_rows), (query_blocks, grad_blocks, log_norm, first_rows)
    )
    return (query_grad.reshape(group_rows, head_count, head_dim), key_grad, value_grad)


def local(
    layer_input,
    out_grad,
    kv_grad,
    lengths,
    token_deal,
    attn_gain,
    query_weight,
    key_weight,
    value_weight,
    out_weight,
    mlp_gain,
    gate_weight,
    up_weight,
    down_weight,
):
    own_rows = layer_input.shape[0]
    col_index = lax.axis_index("col")
    group_rows = own_rows * lax.axis_size("col")
    head_dim = key_weight.shape[1]
    (
        gain_one,
        query_copy,
        key_copy,
        value_copy,
        out_copy,
        gain_two,
        gate_copy,
        up_copy,
        down_copy,
    ) = (
        lax.all_gather(attn_gain.astype(jnp.bfloat16), "row", axis=0, tiled=True),
        lax.all_gather(query_weight.astype(jnp.bfloat16), "row", axis=0, tiled=True),
        lax.all_gather(key_weight.astype(jnp.bfloat16), "row", axis=0, tiled=True),
        lax.all_gather(value_weight.astype(jnp.bfloat16), "row", axis=0, tiled=True),
        lax.all_gather(out_weight.astype(jnp.bfloat16), "row", axis=1, tiled=True),
        lax.all_gather(mlp_gain.astype(jnp.bfloat16), "row", axis=0, tiled=True),
        lax.all_gather(gate_weight.astype(jnp.bfloat16), "row", axis=0, tiled=True),
        lax.all_gather(up_weight.astype(jnp.bfloat16), "row", axis=0, tiled=True),
        lax.all_gather(down_weight.astype(jnp.bfloat16), "row", axis=1, tiled=True),
    )
    gain_one = gain_one.astype(jnp.float32)
    gain_two = gain_two.astype(jnp.float32)
    head_count = query_copy.shape[1] // head_dim
    positions, seq_ids, within = sequence_info(lengths[0], group_rows)
    slot_order = token_deal[0]
    inverse = jnp.zeros((group_rows,), jnp.int32).at[slot_order].set(positions)
    slot_pos = within[slot_order]
    own_pos = lax.dynamic_slice_in_dim(slot_pos, col_index * own_rows, own_rows, 0)
    input_rows = layer_input.astype(jnp.float32)
    factor_one, normed_one = norm_parts(input_rows, gain_one)
    normed_own = normed_one.astype(jnp.bfloat16)
    normed_rows, grad_rows = (
        lax.all_gather(normed_own, "col", axis=0, tiled=True),
        lax.all_gather(out_grad, "col", axis=0, tiled=True),
    )
    queries = jnp.dot(normed_rows, query_copy, preferred_element_type=jnp.float32).reshape(
        group_rows, head_count, head_dim
    )
    queries = rotate_pairs(queries, slot_pos, 1.0).astype(jnp.bfloat16)
    key_proj = jnp.dot(normed_rows, key_copy, preferred_element_type=jnp.float32)
    key_rows = rotate_pairs(key_proj[:, None, :], slot_pos, 1.0)[:, 0, :].astype(jnp.bfloat16)
    value_rows = jnp.dot(normed_rows, value_copy, preferred_element_type=jnp.float32).astype(
        jnp.bfloat16
    )
    shared_rows = jnp.concatenate([key_rows, value_rows], axis=1)
    shared_own = lax.dynamic_slice_in_dim(shared_rows, col_index * own_rows, own_rows, 0)
    query_orig = queries[inverse]
    key_orig = key_rows[inverse]
    value_orig = value_rows[inverse]
    mixed_orig, log_norm = attend_forward(query_orig, key_orig, value_orig, seq_ids)
    mixed_slot = mixed_orig[slot_order].reshape(group_rows, head_count * head_dim)
    out_full = lax.all_gather(out_copy, "col", axis=0, tiled=True)
    mixed_own = lax.all_to_all(mixed_slot, "col", split_axis=0, concat_axis=1, tiled=True)
    attended = jnp.dot(mixed_own, out_full, preferred_element_type=jnp.float32)
    middle = input_rows + attended
    factor_two, normed_two = norm_parts(middle, gain_two)
    mlp_rows = lax.all_gather(normed_two.astype(jnp.bfloat16), "col", axis=0, tiled=True)
    gate_act = jnp.dot(mlp_rows, gate_copy, preferred_element_type=jnp.float32)
    upward = jnp.dot(mlp_rows, up_copy, preferred_element_type=jnp.float32)
    sigmoid_gate = jax.nn.sigmoid(gate_act)
    silu_gate = gate_act * sigmoid_gate
    hidden = (silu_gate * upward).astype(jnp.bfloat16)
    output_rows = middle + lax.psum_scatter(
        jnp.dot(hidden, down_copy, preferred_element_type=jnp.float32),
        "col",
        scatter_dimension=0,
        tiled=True,
    )
    hidden_grad = jnp.dot(grad_rows, down_copy.T, preferred_element_type=jnp.float32)
    down_wgrad = jnp.dot(hidden.T, grad_rows, preferred_element_type=jnp.float32)
    gate_grad = (
        hidden_grad * upward * sigmoid_gate * (1.0 + gate_act * (1.0 - sigmoid_gate))
    ).astype(jnp.bfloat16)
    up_grad = (hidden_grad * silu_gate).astype(jnp.bfloat16)
    gate_wgrad = jnp.dot(mlp_rows.T, gate_grad, preferred_element_type=jnp.float32)
    up_wgrad = jnp.dot(mlp_rows.T, up_grad, preferred_element_type=jnp.float32)
    normed_two_grad = lax.psum_scatter(
        jnp.dot(gate_grad, gate_copy.T, preferred_element_type=jnp.float32)
        + jnp.dot(up_grad, up_copy.T, preferred_element_type=jnp.float32),
        "col",
        scatter_dimension=0,
        tiled=True,
    )
    middle_part, gain_two_grad = norm_backward(middle, factor_two, gain_two, normed_two_grad)
    middle_grad = out_grad.astype(jnp.float32) + middle_part
    middle_low = middle_grad.astype(jnp.bfloat16)
    middle_rows = lax.all_gather(middle_low, "col", axis=0, tiled=True)
    mixed_grad_slot = jnp.dot(middle_rows, out_copy.T, preferred_element_type=jnp.float32).astype(
        jnp.bfloat16
    )
    out_wgrad = jnp.dot(mixed_slot.T, middle_rows, preferred_element_type=jnp.float32)
    mixed_grad = mixed_grad_slot.reshape(group_rows, head_count, head_dim)[inverse]
    query_grad, key_grad, value_grad = attend_backward(
        query_orig, key_orig, value_orig, seq_ids, mixed_grad, log_norm
    )
    query_grad = (
        rotate_pairs(query_grad[slot_order], slot_pos, -1.0)
        .astype(jnp.bfloat16)
        .reshape(group_rows, head_count * head_dim)
    )
    query_wgrad = jnp.dot(normed_rows.T, query_grad, preferred_element_type=jnp.float32)
    shared_part = jnp.concatenate([key_grad, value_grad], axis=1)[slot_order]
    shared_cols = shared_part.shape[1]
    grad_parts = jnp.concatenate(
        [jnp.dot(query_grad, query_copy.T, preferred_element_type=jnp.float32), shared_part], axis=1
    )
    summed_parts = lax.psum_scatter(grad_parts, "col", scatter_dimension=0, tiled=True)
    width_cols = summed_parts.shape[1] - shared_cols
    normed_one_grad = summed_parts[:, :width_cols]
    shared_grad = summed_parts[:, width_cols:]
    shared_grad = shared_grad + kv_grad.astype(jnp.float32)
    key_own = rotate_pairs(shared_grad[:, None, :head_dim], own_pos, -1.0)[:, 0, :].astype(
        jnp.bfloat16
    )
    value_own = shared_grad[:, head_dim:].astype(jnp.bfloat16)
    key_wgrad = jnp.dot(normed_own.T, key_own, preferred_element_type=jnp.float32)
    value_wgrad = jnp.dot(normed_own.T, value_own, preferred_element_type=jnp.float32)
    normed_one_grad = (
        normed_one_grad
        + jnp.dot(key_own, key_copy.T, preferred_element_type=jnp.float32)
        + jnp.dot(value_own, value_copy.T, preferred_element_type=jnp.float32)
    )
    input_part, gain_one_grad = norm_backward(input_rows, factor_one, gain_one, normed_one_grad)
    input_grad = middle_grad + input_part
    summed = (
        lax.psum_scatter(gain_one_grad, "row", scatter_dimension=0, tiled=True),
        lax.psum_scatter(query_wgrad, "row", scatter_dimension=0, tiled=True),
        lax.psum_scatter(key_wgrad, "row", scatter_dimension=0, tiled=True),
        lax.psum_scatter(value_wgrad, "row", scatter_dimension=0, tiled=True),
        lax.psum_scatter(out_wgrad, "row", scatter_dimension=1, tiled=True),
        lax.psum_scatter(gain_two_grad, "row", scatter_dimension=0, tiled=True),
        lax.psum_scatter(gate_wgrad, "row", scatter_dimension=0, tiled=True),
        lax.psum_scatter(up_wgrad, "row", scatter_dimension=0, tiled=True),
        lax.psum_scatter(down_wgrad, "row", scatter_dimension=1, tiled=True),
    )
    gain_one_sum, key_sum, value_sum, gain_two_sum = lax.psum(
        (summed[0], summed[2], summed[3], summed[5]), "col"
    )
    return (
        output_rows.astype(jnp.bfloat16),
        input_grad,
        shared_own,
        gain_one_sum,
        summed[1],
        key_sum,
        value_sum,
        summed[4],
        gain_two_sum,
        summed[6],
        summed[7],
        summed[8],
    )


def solution(mesh):
    in_specs = (
        P(("row", "col"), None),
        P(("row", "col"), None),
        P(("row", "col"), None),
        P("row", None),
        P("row", None),
        P("row"),
        P("row", "col"),
        P("row", None),
        P("row", None),
        P("col", "row"),
        P("row"),
        P("row", "col"),
        P("row", "col"),
        P("col", "row"),
    )
    out_specs = (
        P(("row", "col"), None),
        P(("row", "col"), None),
        P(("row", "col"), None),
        P("row"),
        P("row", "col"),
        P("row", None),
        P("row", None),
        P("col", "row"),
        P("row"),
        P("row", "col"),
        P("row", "col"),
        P("col", "row"),
    )
    return jax.shard_map(local, mesh=mesh, in_specs=in_specs, out_specs=out_specs, check_vma=False)
```

profile of v0, /device:TPU:0, one launch (start us, length us, event | category | flops | bytes accessed | tf_op | source)
XLA Modules:
  0.0 1775.5 jit_solution(17734194517630113278)
XLA Ops:
  24.0 15.5 all-gather.17.cloned.1.call-done
  86.4 37.8 %all-gather.13.cloned.1.call-done = bf16[2048,2048]{0,1:T(8,128)(2,1)} async-done(((bf16[256,2048]{0,1:T(8,128)(2,1)}), bf16[2048,2048]{0,1:T(8,128)(2,1)}) %all-gather.13.cloned.1.call-update) | async-done | bytes 8388624 | tf_op jit(solution)/shard_map/all_gather | solution.py:178
  189.1 50.7 %while.27 = (s32[]{:T(128)}, bf16[4,512,2,128]{3,1,0,2:T(8,128)(2,1)}, f32[4,2,512]{2,1,0:T(2,128)S(1)}, s32[4]{0:T(128)S(1)}, s32[2048]{0:T(1024)S(1)}, /*index...) while((s32[]{:T(128)}, ...), condition=%wide.region_8.9_spmd, body=%wide.region_5.8_spmd.sunk | while | flops 1102183936 | bytes 30984376 | solution.py:80
  243.9 15.1 gather_fusion.4
  276.7 18.2 %all-to-all-done = bf16[8,256,256]{1,2,0:T(8,128)(2,1)S(1)} async-done(((bf16[8,256,256]{1,2,0:T(8,128)(2,1)}), bf16[8,256,256]{1,2,0:T(8,128)(2,1)S(1)}, u32[]{:S(2)}, u32[]{:S(2)}) %all-to-all-start) | async-done | bytes 1048608 | tf_op jit(solution)/shard_map/all_to_all | solution.py:198
  310.7 74.6 %all-gather.21.cloned.1.call-done = bf16[2048,2048]{0,1:T(8,128)(2,1)} async-done(((bf16[256,2048]{0,1:T(8,128)(2,1)}), bf16[2048,2048]{0,1:T(8,128)(2,1)}) %all-gather.21.cloned.1.call-update) | async-done | bytes 8388624 | tf_op jit(solution)/shard_map/all_gather | solution.py:202
  396.3 31.1 %all-gather.25.cloned.1.call-done = bf16[2048,704]{0,1:T(8,128)(2,1)} async-done(((bf16[512,704]{0,1:T(8,128)(2,1)}), bf16[2048,704]{0,1:T(8,128)(2,1)}) %all-gather.25.cloned.1.call-update) | async-done | bytes 2883600 | tf_op jit(solution)/shard_map/all_gather | solution.py:163
  438.5 32.4 %all-gather.27.cloned.1.call-done = bf16[704,2048]{1,0:T(8,128)(2,1)} async-done(((bf16[704,512]{1,0:T(8,128)(2,1)}), bf16[704,2048]{1,0:T(8,128)(2,1)}) %all-gather.27.cloned.1.call-update) | async-done | bytes 2883600 | tf_op jit(solution)/shard_map/all_gather | solution.py:164
  470.8 83.7 %all-gather.29.cloned.1.call-done = bf16[2048,2048]{1,0:T(8,128)(2,1)} async-done(((bf16[256,2048]{1,0:T(8,128)(2,1)}), bf16[2048,2048]{1,0:T(8,128)(2,1)}) %all-gather.29.cloned.1.call-update) | async-done | bytes 8388624 | tf_op jit(solution)/shard_map/all_gather | solution.py:179
  554.5 15.3 multiply_convert_fusion
  595.7 165.2 %reduce-scatter.13.cloned.1.call-done = f32[256,2048]{0,1:T(8,128)} async-done(((f32[2048,2048]{0,1:T(8,128)}), f32[256,2048]{0,1:T(8,128)}) %reduce-scatter.13.cloned.1.call-update) | async-done | bytes 2097168 | tf_op jit(solution)/shard_map/reduce_scatter | solution.py:222
  765.8 81.0 %all-gather.31.cloned.1.call-done = bf16[2048,2048]{0,1:T(8,128)(2,1)} async-done(((bf16[256,2048]{0,1:T(8,128)(2,1)}), bf16[2048,2048]{0,1:T(8,128)(2,1)}) %all-gather.31.cloned.1.call-update) | async-done | bytes 8388624 | tf_op jit(solution)/shard_map/all_gather | solution.py:232
  857.8 15.1 gather_fusion.5
  873.0 77.5 %while.28 = (s32[]{:T(128)}, f32[2048,128]{1,0:T(8,128)S(1)}, f32[2048,128]{1,0:T(8,128)}, f32[4,512,2,128]{3,1,0,2:T(8,128)}, s32[4]{0:T(128)S(1)}, /*index=5*/...) while((s32[]{:T(128)}, f32[2048,128]{1,0:T(8,128)S(1)}, ...), condition=%wide.region_15.16_spmd.clone, body=%wide.region_13.15_spmd.clone.sunk | while | flops 2720398848 | bytes 83409176 | solution.py:119
  955.3 14.5 gather_fusion.6
  1007.6 184.5 %reduce-scatter.15.cloned.1.call-done = f32[256,2304]{0,1:T(8,128)} async-done(((f32[2048,2304]{0,1:T(8,128)}), f32[256,2304]{0,1:T(8,128)}) %reduce-scatter.15.cloned.1.call-update) | async-done | bytes 2359312 | tf_op jit(solution)/shard_map/reduce_scatter | solution.py:252
  1267.7 154.9 %reduce-scatter.11.cloned.1.call-done = f32[256,2048]{0,1:T(8,128)} async-done(((f32[2048,2048]{0,1:T(8,128)}), f32[256,2048]{0,1:T(8,128)}) %reduce-scatter.11.cloned.1.call-update) | async-done | bytes 2097168 | tf_op jit(solution)/shard_map/reduce_scatter | solution.py:208
  1427.5 17.1 all-reduce.4
  1463.3 27.2 %reduce-scatter.29.cloned.1.call-done = f32[704,512]{1,0:T(8,128)} async-done(((f32[704,2048]{1,0:T(8,128)}), f32[704,512]{1,0:T(8,128)}) %reduce-scatter.29.cloned.1.call-update) | async-done | bytes 1441808 | tf_op jit(solution)/shard_map/reduce_scatter | solution.py:279
  1490.4 69.1 %reduce-scatter.25.cloned.1.call-done = f32[512,704]{0,1:T(8,128)} async-done(((f32[2048,704]{0,1:T(8,128)}), f32[512,704]{0,1:T(8,128)}) %reduce-scatter.25.cloned.1.call-update) | async-done | bytes 1441808 | tf_op jit(solution)/shard_map/reduce_scatter | solution.py:277
  1559.5 69.1 %reduce-scatter.27.cloned.1.call-done = f32[512,704]{0,1:T(8,128)} async-done(((f32[2048,704]{0,1:T(8,128)}), f32[512,704]{0,1:T(8,128)}) %reduce-scatter.27.cloned.1.call-update) | async-done | bytes 1441808 | tf_op jit(solution)/shard_map/reduce_scatter | solution.py:278
  1628.7 38.8 %reduce-scatter.17.cloned.1.call-done = f32[512,256]{1,0:T(8,128)} async-done(((f32[2048,256]{1,0:T(8,128)}), f32[512,256]{1,0:T(8,128)}) %reduce-scatter.17.cloned.1.call-update) | async-done | bytes 524304 | tf_op jit(solution)/shard_map/reduce_scatter | solution.py:272
  1667.4 38.6 %reduce-scatter.23.cloned.1.call-done = f32[256,512]{1,0:T(8,128)} async-done(((f32[256,2048]{1,0:T(8,128)}), f32[256,512]{1,0:T(8,128)}) %reduce-scatter.23.cloned.1.call-update) | async-done | bytes 524304 | tf_op jit(solution)/shard_map/reduce_scatter | solution.py:275
  1706.0 59.0 %all-reduce.7.cloned.1.call-done = (f32[512,128]{1,0:T(8,128)}, f32[512,128]{1,0:T(8,128)}) async-done(((f32[512,128]{1,0:T(8,128)}, f32[512,128]{1,0:T(8,128)}), (f32[512,128]{1,0:T(8,128)}, f32[512,128]{1,0:T(8,128)})) %all-reduce.7.cloned.1.call-update) | async-done | bytes 524304 | tf_op jit(solution)/shard_map/psum | solution.py:281
  (369 shorter events, 485.3 us)
Async XLA Ops:
  7.2 32.3 %all-gather.17.cloned.1.call-start = ((), (), s32[]{:S(2)}) async-start(), calls=%async_computation.13 | async-start | bytes 1310720 | tf_op jit(solution)/shard_map/all_gather | solution.py:160
  9.0 115.2 %all-gather.13.cloned.1.call-start = ((), (), s32[]{:S(2)}) async-start(), calls=%async_computation.11 | async-start | bytes 9437184 | tf_op jit(solution)/shard_map/all_gather | solution.py:178
  23.2 128.1 %all-gather.15.cloned.1.call-start = ((), (), s32[]{:S(2)}) async-start(), calls=%async_computation.12 | async-start | bytes 1310720 | tf_op jit(solution)/shard_map/all_gather | solution.py:157
  24.0 252.7 %all-gather.19.cloned.1.call-start = ((), (), s32[]{:S(2)}) async-start(), calls=%async_computation.14 | async-start | bytes 9437184 | tf_op jit(solution)/shard_map/all_gather | solution.py:197
  39.5 271.1 %all-gather.23.cloned.1.call-start = ((), (), s32[]{:S(2)}) async-start(), calls=%async_computation.16 | async-start | bytes 3604480 | tf_op jit(solution)/shard_map/all_gather | solution.py:162
  263.8 31.2 %all-to-all-start = ((bf16[8,256,256]{1,2,0:T(8,128)(2,1)}), bf16[8,256,256]{1,2,0:T(8,128)(2,1)S(1)}, u32[]{:S(2)}, u32[]{:S(2)}) async-start(bf16[8,256,256]{1,2,0:T(8,128)(2,1)} %copy.124), calls=%async_computation | async-start | bytes 2097152 | tf_op jit(solution)/shard_map/all_to_all | solution.py:198
  268.4 116.9 %all-gather.21.cloned.1.call-start = ((), (), s32[]{:S(2)}) async-start(), calls=%async_computation.15 | async-start | bytes 9437184 | tf_op jit(solution)/shard_map/all_gather | solution.py:202
  276.7 487.3 %copy-start.34 = (f32[4,1,512]{2,1,0:T(1,128)}, f32[4,1,512]{2,1,0:T(1,128)S(1)}, u32[]{:S(2)}) copy-start(f32[4,1,512]{2,1,0:T(1,128)S(1)} %convert_element_type.144) | copy-start | bytes 24580
  303.0 460.9 %copy-start = (f32[256,2048]{0,1:T(8,128)}, f32[256,2048]{0,1:T(8,128)S(1)}, u32[]{:S(2)}) copy-start(f32[256,2048]{0,1:T(8,128)S(1)} %get-tuple-element.395) | copy-start | bytes 6291460
  304.7 122.8 %all-gather.25.cloned.1.call-start = ((), (), s32[]{:S(2)}) async-start(), calls=%async_computation.17 | async-start | bytes 3604480 | tf_op jit(solution)/shard_map/all_gather | solution.py:163
  307.1 163.8 %all-gather.27.cloned.1.call-start = ((), (), s32[]{:S(2)}) async-start(), calls=%async_computation.18 | async-start | bytes 3604480 | tf_op jit(solution)/shard_map/all_gather | solution.py:164
  309.8 244.7 %all-gather.29.cloned.1.call-start = ((), (), s32[]{:S(2)}) async-start(), calls=%async_computation.20 | async-start | bytes 9437184 | tf_op jit(solution)/shard_map/all_gather | solution.py:179
  310.6 450.3 %reduce-scatter.13.cloned.1.call-start = ((), (), s32[]{:S(2)}) async-start(), calls=%async_computation.21 | async-start | bytes 18874368 | tf_op jit(solution)/shard_map/reduce_scatter | solution.py:222
  594.1 252.7 %all-gather.31.cloned.1.call-start = ((), (), s32[]{:S(2)}) async-start(), calls=%async_computation.22 | async-start | bytes 9437184 | tf_op jit(solution)/shard_map/all_gather | solution.py:232
  765.7 426.4 %reduce-scatter.15.cloned.1.call-start = ((), (), s32[]{:S(2)}) async-start(), calls=%async_computation.23 | async-start | bytes 21233664 | tf_op jit(solution)/shard_map/reduce_scatter | solution.py:252
  1005.9 261.8 %reduce-scatter.19.cloned.1.call-start = ((), (), s32[]{:S(2)}) async-start(), calls=%async_computation.25 | async-start | bytes 1310720 | tf_op jit(solution)/shard_map/reduce_scatter | solution.py:273
  1194.9 72.7 %reduce-scatter.21.cloned.1.call-start = ((), (), s32[]{:S(2)}) async-start(), calls=%async_computation.26 | async-start | bytes 1310720 | tf_op jit(solution)/shard_map/reduce_scatter | solution.py:274
  1196.4 226.1 %reduce-scatter.11.cloned.1.call-start = ((), (), s32[]{:S(2)}) async-start(), calls=%async_computation.19 | async-start | bytes 18874368 | tf_op jit(solution)/shard_map/reduce_scatter | solution.py:208
  1209.2 281.2 %reduce-scatter.29.cloned.1.call-start = ((), (), s32[]{:S(2)}) async-start(), calls=%async_computation.30 | async-start | bytes 7208960 | tf_op jit(solution)/shard_map/reduce_scatter | solution.py:279
  1220.4 339.1 %reduce-scatter.25.cloned.1.call-start = ((), (), s32[]{:S(2)}) async-start(), calls=%async_computation.28 | async-start | bytes 7208960 | tf_op jit(solution)/shard_map/reduce_scatter | solution.py:277
  1231.7 396.9 %reduce-scatter.27.cloned.1.call-start = ((), (), s32[]{:S(2)}) async-start(), calls=%async_computation.29 | async-start | bytes 7208960 | tf_op jit(solution)/shard_map/reduce_scatter | solution.py:278
  1243.0 424.5 %reduce-scatter.17.cloned.1.call-start = ((), (), s32[]{:S(2)}) async-start(), calls=%async_computation.24 | async-start | bytes 2621440 | tf_op jit(solution)/shard_map/reduce_scatter | solution.py:272
  1250.5 455.5 %reduce-scatter.23.cloned.1.call-start = ((), (), s32[]{:S(2)}) async-start(), calls=%async_computation.27 | async-start | bytes 2621440 | tf_op jit(solution)/shard_map/reduce_scatter | solution.py:275
  1260.1 505.0 %all-reduce.7.cloned.1.call-start = ((), (), s32[]{:S(2)}) async-start(), calls=%async_computation.31 | async-start | bytes 1048576 | tf_op jit(solution)/shard_map/psum | solution.py:281
  (65 other events, 2976.5 us)
Sparse Core Ops, SparseCore 0:
  10.4 29.0 all-gather.16
  41.7 82.4 all-gather.12
  126.6 24.6 all-gather.14
  152.8 82.0 all-gather.18
  236.5 40.0 all-gather.22
  304.8 80.4 all-gather.20
  387.7 39.7 all-gather.24
  429.3 41.5 all-gather.26
  472.4 82.0 all-gather.28
  594.2 166.6 reduce-scatter.12
  765.8 80.9 all-gather.30
  1006.0 186.0 reduce-scatter.14
  1195.0 26.3 reduce-scatter.18
  1224.2 27.9 reduce-scatter.20
  1254.4 168.1 reduce-scatter.10
  1426.0 64.4 reduce-scatter.28
  1493.8 65.6 reduce-scatter.24
  1563.0 65.6 reduce-scatter.26
  1632.2 35.1 reduce-scatter.16
  1670.8 35.1 reduce-scatter.22
  1708.4 56.5 all-reduce.6
where the time goes:
time: 1780 us
  waiting for transfers between devices  1180 us (66%)
  matrix products  230 us (13%)
  local copies, waits for them, and re-layouts  159 us (9%)
  other arithmetic  96.3 us (5%)
  blocking collectives  68.7 us (4%)
    reduce_scatter x1, waiting for transfers between devices, local(): lax.psum_scatter(grad_parts, 'col', scatter_dimension=0, tiled=True)  184 us
    reduce_scatter x1, waiting for transfers between devices, local(): lax.psum_scatter(jnp.dot(gate_grad, gate_copy.T, preferred_element_type=j...  165 us
    reduce_scatter x1, waiting for transfers between devices, local(): lax.psum_scatter(jnp.dot(hidden, down_copy, preferred_element_type=jnp.fl...  155 us
    all_gather x1, waiting for transfers between devices, local(): lax.all_gather(out_grad, 'col', axis=0, tiled=True)  83.7 us
    all_gather x1, waiting for transfers between devices, local(): middle_rows = lax.all_gather(middle_low, 'col', axis=0, tiled=True)  81 us
    all_gather x1, waiting for transfers between devices, local(): lax.all_gather(normed_two.astype(jnp.bfloat16), 'col', axis=0, tiled=True)  74.6 us
    reduce_scatter x1, waiting for transfers between devices, local(): lax.psum_scatter(up_wgrad, 'row', scatter_dimension=0, tiled=True)  69.1 us
    reduce_scatter x1, waiting for transfers between devices, local(): lax.psum_scatter(gate_wgrad, 'row', scatter_dimension=0, tiled=True)  69.1 us
  transfers between devices with their start and end apart: 22, of which 18 were waited for; matrix products, arithmetic and copies ran while one was open for 16% of the time, Pallas kernels for 0%

commit v1 on v0

--- a/solution.py
+++ b/solution.py
@@ -6,6 +6,12 @@
 norm_eps = 1e-05
 rope_base = 10000.0
 masked_score = -1e30
+
+
+def in_order(blocks, dim):
+    shape = list(blocks.shape[1:])
+    shape[dim] *= blocks.shape[0]
+    return jnp.moveaxis(blocks, 0, dim).reshape(shape)
 
 
 def rotate_pairs(values, positions, direction):
@@ -229,7 +235,14 @@
     middle_part, gain_two_grad = norm_backward(middle, factor_two, gain_two, normed_two_grad)
     middle_grad = out_grad.astype(jnp.float32) + middle_part
     middle_low = middle_grad.astype(jnp.bfloat16)
-    middle_rows = lax.all_gather(middle_low, "col", axis=0, tiled=True)
+    size = lax.axis_size("col")
+    right = [(i, (i + 1) % size) for i in range(size)]
+    pieces_2 = [middle_low]
+    while len(pieces_2) < size:
+        pieces_2.append(lax.ppermute(pieces_2[-1], "col", right))
+    here = lax.axis_index("col")
+    pieces_2 = jnp.stack(pieces_2)[(here - jnp.arange(size)) % size]
+    middle_rows = in_order(pieces_2, 0)
     mixed_grad_slot = jnp.dot(middle_rows, out_copy.T, preferred_element_type=jnp.float32).astype(
         jnp.bfloat16
     )

time: 1780 us -> 1830 us (1.028)
  local copies, waits for them, and re-layouts: 159 us -> 189 us
  waiting for transfers between devices: 1180 us -> 1210 us
    ppermute x0 -> x7, waiting for transfers between devices: none -> 104 us  [local(): pieces_2.append(lax.ppermute(pieces_2[-1], 'col', right))]
    all_gather x1 -> x0, waiting for transfers between devices: 81 us -> none  [local(): middle_rows = lax.all_gather(middle_low, 'col', axis=0, tiled=True)]
    gather x0 -> x2, local copies, waits for them, and re-layouts: none -> 19.7 us  [local(): pieces_2 = jnp.stack(pieces_2)[(here - jnp.arange(size)) % size]]
  transfers between devices with their start and end apart: 22 -> 28, of which waited for: 18 -> 24; matrix products, arithmetic and copies ran while one was open for 16% -> 16% of each run, Pallas kernels for 0% -> 0%
where the time goes in v1:
time: 1830 us
  waiting for transfers between devices  1210 us (66%)
  matrix products  229 us (13%)
  local copies, waits for them, and re-layouts  189 us (10%)
  other arithmetic  96.4 us (5%)
  blocking collectives  68.6 us (4%)
    reduce_scatter x1, waiting for transfers between devices, local(): lax.psum_scatter(grad_parts, 'col', scatter_dimension=0, tiled=True)  184 us
    reduce_scatter x1, waiting for transfers between devices, local(): lax.psum_scatter(jnp.dot(gate_grad, gate_copy.T, preferred_element_type=j...  165 us
    reduce_scatter x1, waiting for transfers between devices, local(): lax.psum_scatter(jnp.dot(hidden, down_copy, preferred_element_type=jnp.fl...  155 us
    ppermute x7, waiting for transfers between devices, local(): pieces_2.append(lax.ppermute(pieces_2[-1], 'col', right))  104 us
    all_gather x1, waiting for transfers between devices, local(): lax.all_gather(out_grad, 'col', axis=0, tiled=True)  83.7 us
    all_gather x1, waiting for transfers between devices, local(): lax.all_gather(normed_two.astype(jnp.bfloat16), 'col', axis=0, tiled=True)  74.6 us
    reduce_scatter x1, waiting for transfers between devices, local(): lax.psum_scatter(gate_wgrad, 'row', scatter_dimension=0, tiled=True)  69.1 us
    reduce_scatter x1, waiting for transfers between devices, local(): lax.psum_scatter(up_wgrad, 'row', scatter_dimension=0, tiled=True)  69.1 us
  transfers between devices with their start and end apart: 28, of which 24 were waited for; matrix products, arithmetic and copies ran while one was open for 16% of the time, Pallas kernels for 0%

profile of v1, /device:TPU:0, one launch (start us, length us, event | category | flops | bytes accessed | tf_op | source)
XLA Modules:
  0.0 1827.7 jit_solution(3670408259329383800)
XLA Ops:
  24.0 15.5 all-gather.16.cloned.1.call-done
  86.5 37.7 %all-gather.12.cloned.1.call-done = bf16[2048,2048]{0,1:T(8,128)(2,1)} async-done(((bf16[256,2048]{0,1:T(8,128)(2,1)}), bf16[2048,2048]{0,1:T(8,128)(2,1)}) %all-gather.12.cloned.1.call-update) | async-done | bytes 8388624 | tf_op jit(solution)/shard_map/all_gather | solution.py:184
  189.1 50.7 %while.27 = (s32[]{:T(128)}, bf16[4,512,2,128]{3,1,0,2:T(8,128)(2,1)}, f32[4,2,512]{2,1,0:T(2,128)S(1)}, s32[4]{0:T(128)S(1)}, s32[2048]{0:T(1024)S(1)}, /*index...) while((s32[]{:T(128)}, ...), condition=%wide.region_8.9_spmd, body=%wide.region_5.8_spmd.sunk | while | flops 1102183936 | bytes 30984376 | solution.py:86
  276.7 18.2 all-to-all-done
  310.7 74.6 %all-gather.20.cloned.1.call-done = bf16[2048,2048]{0,1:T(8,128)(2,1)} async-done(((bf16[256,2048]{0,1:T(8,128)(2,1)}), bf16[2048,2048]{0,1:T(8,128)(2,1)}) %all-gather.20.cloned.1.call-update) | async-done | bytes 8388624 | tf_op jit(solution)/shard_map/all_gather | solution.py:208
  396.3 31.1 %all-gather.24.cloned.1.call-done = bf16[2048,704]{0,1:T(8,128)(2,1)} async-done(((bf16[512,704]{0,1:T(8,128)(2,1)}), bf16[2048,704]{0,1:T(8,128)(2,1)}) %all-gather.24.cloned.1.call-update) | async-done | bytes 2883600 | tf_op jit(solution)/shard_map/all_gather | solution.py:169
  438.5 32.4 %all-gather.26.cloned.1.call-done = bf16[704,2048]{1,0:T(8,128)(2,1)} async-done(((bf16[704,512]{1,0:T(8,128)(2,1)}), bf16[704,2048]{1,0:T(8,128)(2,1)}) %all-gather.26.cloned.1.call-update) | async-done | bytes 2883600 | tf_op jit(solution)/shard_map/all_gather | solution.py:170
  470.8 83.7 %all-gather.28.cloned.1.call-done = bf16[2048,2048]{1,0:T(8,128)(2,1)} async-done(((bf16[256,2048]{1,0:T(8,128)(2,1)}), bf16[2048,2048]{1,0:T(8,128)(2,1)}) %all-gather.28.cloned.1.call-update) | async-done | bytes 8388624 | tf_op jit(solution)/shard_map/all_gather | solution.py:185
  595.6 165.3 %reduce-scatter.13.cloned.1.call-done = f32[256,2048]{0,1:T(8,128)} async-done(((f32[2048,2048]{0,1:T(8,128)}), f32[256,2048]{0,1:T(8,128)}) %reduce-scatter.13.cloned.1.call-update) | async-done | bytes 2097168 | tf_op jit(solution)/shard_map/reduce_scatter | solution.py:228
  765.6 16.0 collective-permute-done
  781.7 16.0 collective-permute-done.1
  797.7 16.0 collective-permute-done.2
  813.7 16.1 collective-permute-done.3
  829.9 16.3 collective-permute-done.4
  925.0 77.7 %while.28 = (s32[]{:T(128)}, f32[2048,128]{1,0:T(8,128)S(1)}, f32[2048,128]{1,0:T(8,128)}, f32[4,512,2,128]{3,1,0,2:T(8,128)}, s32[4]{0:T(128)S(1)}, /*index=5*/...) while((s32[]{:T(128)}, f32[2048,128]{1,0:T(8,128)S(1)}, ...), condition=%wide.region_15.16_spmd.clone, body=%wide.region_13.15_spmd.clone.sunk | while | flops 2720398848 | bytes 83409176 | solution.py:125
  1059.9 184.5 %reduce-scatter.15.cloned.1.call-done = f32[256,2304]{0,1:T(8,128)} async-done(((f32[2048,2304]{0,1:T(8,128)}), f32[256,2304]{0,1:T(8,128)}) %reduce-scatter.15.cloned.1.call-update) | async-done | bytes 2359312 | tf_op jit(solution)/shard_map/reduce_scatter | solution.py:265
  1319.7 155.3 %reduce-scatter.11.cloned.1.call-done = f32[256,2048]{0,1:T(8,128)} async-done(((f32[2048,2048]{0,1:T(8,128)}), f32[256,2048]{0,1:T(8,128)}) %reduce-scatter.11.cloned.1.call-update) | async-done | bytes 2097168 | tf_op jit(solution)/shard_map/reduce_scatter | solution.py:214
  1479.9 17.1 all-reduce.4
  1515.7 27.2 %reduce-scatter.29.cloned.1.call-done = f32[704,512]{1,0:T(8,128)} async-done(((f32[704,2048]{1,0:T(8,128)}), f32[704,512]{1,0:T(8,128)}) %reduce-scatter.29.cloned.1.call-update) | async-done | bytes 1441808 | tf_op jit(solution)/shard_map/reduce_scatter | solution.py:292
  1542.8 69.1 %reduce-scatter.25.cloned.1.call-done = f32[512,704]{0,1:T(8,128)} async-done(((f32[2048,704]{0,1:T(8,128)}), f32[512,704]{0,1:T(8,128)}) %reduce-scatter.25.cloned.1.call-update) | async-done | bytes 1441808 | tf_op jit(solution)/shard_map/reduce_scatter | solution.py:290
  1612.0 69.1 %reduce-scatter.27.cloned.1.call-done = f32[512,704]{0,1:T(8,128)} async-done(((f32[2048,704]{0,1:T(8,128)}), f32[512,704]{0,1:T(8,128)}) %reduce-scatter.27.cloned.1.call-update) | async-done | bytes 1441808 | tf_op jit(solution)/shard_map/reduce_scatter | solution.py:291
  1681.1 38.6 %reduce-scatter.17.cloned.1.call-done = f32[512,256]{1,0:T(8,128)} async-done(((f32[2048,256]{1,0:T(8,128)}), f32[512,256]{1,0:T(8,128)}) %reduce-scatter.17.cloned.1.call-update) | async-done | bytes 524304 | tf_op jit(solution)/shard_map/reduce_scatter | solution.py:285
  1719.7 38.7 %reduce-scatter.23.cloned.1.call-done = f32[256,512]{1,0:T(8,128)} async-done(((f32[256,2048]{1,0:T(8,128)}), f32[256,512]{1,0:T(8,128)}) %reduce-scatter.23.cloned.1.call-update) | async-done | bytes 524304 | tf_op jit(solution)/shard_map/reduce_scatter | solution.py:288
  1758.4 58.9 %all-reduce.7.cloned.1.call-done = (f32[512,128]{1,0:T(8,128)}, f32[512,128]{1,0:T(8,128)}) async-done(((f32[512,128]{1,0:T(8,128)}, f32[512,128]{1,0:T(8,128)}), (f32[512,128]{1,0:T(8,128)}, f32[512,128]{1,0:T(8,128)})) %all-reduce.7.cloned.1.call-update) | async-done | bytes 524304 | tf_op jit(solution)/shard_map/psum | solution.py:294
  (397 shorter events, 597.8 us)
Async XLA Ops:
  7.2 32.3 %all-gather.16.cloned.1.call-start = ((), (), s32[]{:S(2)}) async-start(), calls=%async_computation.13 | async-start | bytes 1310720 | tf_op jit(solution)/shard_map/all_gather | solution.py:166
  9.0 115.2 %all-gather.12.cloned.1.call-start = ((), (), s32[]{:S(2)}) async-start(), calls=%async_computation.11 | async-start | bytes 9437184 | tf_op jit(solution)/shard_map/all_gather | solution.py:184
  23.2 128.1 %all-gather.14.cloned.1.call-start = ((), (), s32[]{:S(2)}) async-start(), calls=%async_computation.12 | async-start | bytes 1310720 | tf_op jit(solution)/shard_map/all_gather | solution.py:163
  24.0 252.7 %all-gather.18.cloned.1.call-start = ((), (), s32[]{:S(2)}) async-start(), calls=%async_computation.14 | async-start | bytes 9437184 | tf_op jit(solution)/shard_map/all_gather | solution.py:203
  39.5 271.1 %all-gather.22.cloned.1.call-start = ((), (), s32[]{:S(2)}) async-start(), calls=%async_computation.16 | async-start | bytes 3604480 | tf_op jit(solution)/shard_map/all_gather | solution.py:168
  263.8 31.2 %all-to-all-start = ((bf16[8,256,256]{1,2,0:T(8,128)(2,1)}), bf16[8,256,256]{1,2,0:T(8,128)(2,1)S(1)}, u32[]{:S(2)}, u32[]{:S(2)}) async-start(bf16[8,256,256]{1,2,0:T(8,128)(2,1)} %copy.156), calls=%async_computation | async-start | bytes 2097152 | tf_op jit(solution)/shard_map/all_to_all | solution.py:204
  268.4 116.9 %all-gather.20.cloned.1.call-start = ((), (), s32[]{:S(2)}) async-start(), calls=%async_computation.15 | async-start | bytes 9437184 | tf_op jit(solution)/shard_map/all_gather | solution.py:208
  304.7 122.8 %all-gather.24.cloned.1.call-start = ((), (), s32[]{:S(2)}) async-start(), calls=%async_computation.17 | async-start | bytes 3604480 | tf_op jit(solution)/shard_map/all_gather | solution.py:169
  307.0 163.8 %all-gather.26.cloned.1.call-start = ((), (), s32[]{:S(2)}) async-start(), calls=%async_computation.18 | async-start | bytes 3604480 | tf_op jit(solution)/shard_map/all_gather | solution.py:170
  309.9 244.6 %all-gather.28.cloned.1.call-start = ((), (), s32[]{:S(2)}) async-start(), calls=%async_computation.20 | async-start | bytes 9437184 | tf_op jit(solution)/shard_map/all_gather | solution.py:185
  310.6 450.3 %reduce-scatter.13.cloned.1.call-start = ((), (), s32[]{:S(2)}) async-start(), calls=%async_computation.21 | async-start | bytes 18874368 | tf_op jit(solution)/shard_map/reduce_scatter | solution.py:228
  594.1 650.3 %reduce-scatter.15.cloned.1.call-start = ((), (), s32[]{:S(2)}) async-start(), calls=%async_computation.22 | async-start | bytes 21233664 | tf_op jit(solution)/shard_map/reduce_scatter | solution.py:265
  813.7 16.1 collective-permute-start.3
  829.8 16.3 collective-permute-start.4
  846.2 16.2 collective-permute-start.5
  1058.2 261.5 %reduce-scatter.19.cloned.1.call-start = ((), (), s32[]{:S(2)}) async-start(), calls=%async_computation.24 | async-start | bytes 1310720 | tf_op jit(solution)/shard_map/reduce_scatter | solution.py:286
  1247.1 72.5 %reduce-scatter.21.cloned.1.call-start = ((), (), s32[]{:S(2)}) async-start(), calls=%async_computation.25 | async-start | bytes 1310720 | tf_op jit(solution)/shard_map/reduce_scatter | solution.py:287
  1248.6 226.3 %reduce-scatter.11.cloned.1.call-start = ((), (), s32[]{:S(2)}) async-start(), calls=%async_computation.19 | async-start | bytes 18874368 | tf_op jit(solution)/shard_map/reduce_scatter | solution.py:214
  1261.4 281.4 %reduce-scatter.29.cloned.1.call-start = ((), (), s32[]{:S(2)}) async-start(), calls=%async_computation.29 | async-start | bytes 7208960 | tf_op jit(solution)/shard_map/reduce_scatter | solution.py:292
  1272.6 339.3 %reduce-scatter.25.cloned.1.call-start = ((), (), s32[]{:S(2)}) async-start(), calls=%async_computation.27 | async-start | bytes 7208960 | tf_op jit(solution)/shard_map/reduce_scatter | solution.py:290
  1283.9 397.1 %reduce-scatter.27.cloned.1.call-start = ((), (), s32[]{:S(2)}) async-start(), calls=%async_computation.28 | async-start | bytes 7208960 | tf_op jit(solution)/shard_map/reduce_scatter | solution.py:291
  1295.1 424.5 %reduce-scatter.17.cloned.1.call-start = ((), (), s32[]{:S(2)}) async-start(), calls=%async_computation.23 | async-start | bytes 2621440 | tf_op jit(solution)/shard_map/reduce_scatter | solution.py:285
  1302.6 455.8 %reduce-scatter.23.cloned.1.call-start = ((), (), s32[]{:S(2)}) async-start(), calls=%async_computation.26 | async-start | bytes 2621440 | tf_op jit(solution)/shard_map/reduce_scatter | solution.py:288
  1312.1 505.2 %all-reduce.7.cloned.1.call-start = ((), (), s32[]{:S(2)}) async-start(), calls=%async_computation.30 | async-start | bytes 1048576 | tf_op jit(solution)/shard_map/psum | solution.py:294
  (74 other events, 3953.5 us)
Sparse Core Ops, SparseCore 0:
  10.4 29.0 all-gather.15
  41.7 82.4 all-gather.11
  126.6 24.6 all-gather.13
  152.8 82.0 all-gather.17
  236.5 40.0 all-gather.21
  304.8 80.4 all-gather.19
  387.6 39.7 all-gather.23
  429.2 41.5 all-gather.25
  472.4 82.0 all-gather.27
  594.2 166.6 reduce-scatter.12
  1058.3 186.0 reduce-scatter.14
  1247.3 26.4 reduce-scatter.18
  1276.6 27.9 reduce-scatter.20
  1306.8 168.1 reduce-scatter.10
  1478.4 64.4 reduce-scatter.28
  1546.3 65.6 reduce-scatter.24
  1615.4 65.6 reduce-scatter.26
  1684.5 35.1 reduce-scatter.16
  1723.2 35.1 reduce-scatter.22
  1760.7 56.6 all-reduce.6
